TPU v7x, 32 devices: a whole 2x2x4 slice. The times are simulated.
32 devices in a mesh: grp: 4 (over y, x), mem: 8 (over z, core).
Axes of the slice: x: 2, y: 2, z: 4, core: 2. Of those that a mesh axis runs over, the one named last changes fastest.
Arguments:
- weight: bfloat16 [2, 16384, 16384], P(None, None, ('grp', 'mem')), may hold values from -0.046875 to 0.046875
- activation: bfloat16 [2, 16384, 512], P(None, ('grp', 'mem')), may hold values from -6 to 6
- points: int32 [4], replicated, may hold values from 0 to 3, each once
Outputs:
- share: float32 [4, 16384, 512], P('grp', 'mem')
Inputs may be any that keep to these rules, and one draw needn't show every extreme that they name: A permutation of 0 to 3; group g evaluates at points[g] + 1.
All inputs are finite; a program needn't handle non-finite values.
Results may differ from a plain program's by a relative error of at most 0.0042.
Values may be sent and summed in bfloat16 or wider, within the bound.
A program may use at most 320 MiB of HBM per device.

v0:
```python
import jax
import jax.numpy as jnp
from jax import lax
from jax.experimental import pallas as pl
from jax.experimental.pallas import tpu as pltpu
from jax.sharding import PartitionSpec as P

PAIRS = 4
F32, BF16 = jnp.float32, jnp.bfloat16
MESH = pl.DeviceIdType.MESH


def loop(n, body):
    def step(i, carry):
        body(i)
        return carry

    lax.fori_loop(0, n, step, 0)


def make_kernel(groups, members, blocks, splits, rows, depth, cols, ra, rb):
    bits = groups.bit_length() - 1
    ring = members // 2
    half = groups // 2
    off = [groups - (groups >> s) for s in range(bits + 1)]

    def kernel(points, weight, act, out, wxa, wxb, xp, xs, wt, cw, asend, az, ag, bsend, bg, bz,
               x_s, x_r, w_s, wa_r, wb_r, ld, send, az_r, ag_r, bg_r, bz_r):
        me_g = lax.axis_index("grp")
        me_m = lax.axis_index("mem")
        z, core = me_m // 2, me_m % 2
        twin = (me_g, z * 2 + 1 - core)

        def along(sgn):
            return (me_g, ((z + sgn + ring) % ring) * 2 + core)

        def blend(o, v0, v1):
            return v0 + o * (v1 - v0)

        def bit_of(w):
            return (me_g // w) % 2

        def across(o, s):
            w0, w1 = 1 << (bits - 1 - s), 1 << s
            p0 = me_g + w0 - 2 * w0 * bit_of(w0)
            p1 = me_g + w1 - 2 * w1 * bit_of(w1)
            return (blend(o, p0, p1), me_m)

        def group_at(o, s, h, j):
            w0, w1 = 1 << (bits - 1 - s), 1 << s
            b0, b1 = bit_of(w0), bit_of(w1)
            b0, b1 = b0 + h - 2 * b0 * h, b1 + h - 2 * b1 * h
            g0 = (me_g // (2 * w0)) * (2 * w0) + b0 * w0 + j
            g1 = me_g % w1 + b1 * w1 + j * (2 * w1)
            return blend(o, g0, g1)

        def slot_at(o, s, h, j):
            w0, w1 = 1 << (bits - 1 - s), 1 << s
            b0, b1 = bit_of(w0), bit_of(w1)
            b0, b1 = b0 + h - 2 * b0 * h, b1 + h - 2 * b1 * h
            return blend(o, b0 * w0 + j, b1 + 2 * j)

        def remote(src, dst, ssem, rsem, dev):
            return pltpu.make_async_remote_copy(
                src_ref=src, dst_ref=dst, send_sem=ssem, recv_sem=rsem, device_id=dev, device_id_type=MESH)

        def arrived(ref, sem):
            pltpu.make_async_copy(ref, ref, sem).wait()

        def anchor(g):
            return (points[g] + 1).astype(F32) / groups

        def power(a, n):
            r = a
            for _ in range(n - 1):
                r = r * a
            return r

        barrier = pltpu.get_barrier_semaphore()
        peers = [twin, along(1), along(-1)] + [across(0, s) for s in range(bits)]
        for dev in peers:
            pl.semaphore_signal(barrier, inc=1, device_id=dev, device_id_type=MESH)
        pl.semaphore_wait(barrier, len(peers))

        def a_sign(c):
            return 1 - 2 * c

        def b_sign(c):
            return 1 - 2 * ((c % 2 + c // 2) % 2)

        def dest(sgn, t):
            return (z - sgn * (1 + t) + 2 * ring) % ring

        def base(is_a, c, zd, core_):
            lead = c * ra if is_a else 2 * ra + c * rb
            return pl.multiple_of((zd * 2 + core_) * rows + lead, 16)

        x_copy = remote(act, xp, x_s, x_r, twin)
        x_copy.start()

        def push_a(t):
            def body(c):
                zd = dest(a_sign(c), t)
                remote(weight.at[:, pl.ds(base(True, c, zd, 1 - core), ra), :], wxa.at[c, t],
                       w_s.at[0], wa_r.at[c, t], twin).start()
            loop(2, body)

        def push_b(c):
            def body(t):
                zd = dest(b_sign(c), t)
                remote(weight.at[:, pl.ds(base(False, c, zd, 1 - core), rb), :], wxb.at[c, t],
                       w_s.at[1], wb_r.at[c], twin).start()
            loop(ring, body)

        push_b(0)
        push_b(1)
        push_a(0)
        if ring > 2:
            push_a(1)
        loop(2 * PAIRS - 2, lambda c: push_b(c + 2))
        for t in range(2, ring):
            push_a(t)

        step = min(16, depth)
        lifts = [power(anchor(g), blocks) for g in range(groups)]

        def code_input(h, src):
            def body(r):
                at = pl.ds(pl.multiple_of(r * step, step), step)
                to = pl.ds(pl.multiple_of(h * depth + r * step, step), step)
                parts = [src[k, at, :].astype(F32) for k in range(splits)]
                for g in range(groups):
                    total = parts[0]
                    for k in range(1, splits):
                        total = total + power(lifts[g], k) * parts[k]
                    xs[g, to, :] = total.astype(BF16)
            loop(depth // step, body)

        code_input(0, act)
        x_copy.wait_recv()
        code_input(1, xp)

        def tile_copies(is_a, c, t, sgn, slot):
            n = ra if is_a else rb
            wx = wxa if is_a else wxb
            own = pltpu.make_async_copy(
                weight.at[:, pl.ds(base(is_a, c, dest(sgn, t), core), n), :],
                wt.at[slot, 0, :, pl.ds(0, n), :], ld.at[slot, 0])
            other = pltpu.make_async_copy(wx.at[c, t], wt.at[slot, 1, :, pl.ds(0, n), :], ld.at[slot, 1])
            return own, other

        def product(slot, n, g):
            a = anchor(g)
            factors = [power(a, j) for j in range(1, blocks)]

            def body(r):
                at = pl.ds(r * 16, 16)
                for h in range(2):
                    total = wt[slot, h, 0, at, :].astype(F32)
                    for j in range(1, blocks):
                        total = total + factors[j - 1] * wt[slot, h, j, at, :].astype(F32)
                    cw[at, h * depth:(h + 1) * depth] = total.astype(BF16)
            for r in range(n // 16):
                body(r)
            return jnp.dot(cw[0:n, :], xs[g], preferred_element_type=F32)

        def a_hop(t):
            def body(c, slot):
                def per_group(g):
                    acc = product(slot, ra, g)
                    if t == 0:
                        src = asend.at[c, g]
                        asend[c, g] = acc.astype(BF16)
                    else:
                        src = az.at[c, t - 1, g]
                        arrived(src, az_r.at[c, t - 1, g])
                        az[c, t - 1, g] = (acc + az[c, t - 1, g].astype(F32)).astype(BF16)
                    remote(src, az.at[c, t, g], send.at[0 if t == 0 else 1], az_r.at[c, t, g],
                           along(a_sign(c))).start()
                loop(groups, per_group)
            return body

        def a_turn(c, slot):
            def per_group(i):
                h, j = 1 - i // half, i % half
                g = group_at(c, 0, h, j)
                acc = product(slot, ra, g)
                arrived(az.at[c, ring - 2, g], az_r.at[c, ring - 2, g])
                az[c, ring - 2, g] = (acc + az[c, ring - 2, g].astype(F32)).astype(BF16)

                @pl.when(i < half)
                def _():
                    remote(az.at[c, ring - 2, g], ag.at[c, j], send.at[2], ag_r.at[c, 0], across(c, 0)).start()
            loop(groups, per_group)

        def a_stage(s):
            def body(c):
                n = half >> (s - 1)
                arrived(ag.at[c, pl.ds(off[s - 1], n)], ag_r.at[c, s - 1])

                def held(j):
                    if s == 1:
                        return az[c, ring - 2, group_at(c, 0, 0, j)]
                    return ag[c, off[s - 2] + slot_at(c, s - 1, 0, j)]

                def summed(j):
                    return ag[c, off[s - 1] + j].astype(F32) + held(j).astype(F32)

                if s == bits:
                    out[0, pl.ds(pl.multiple_of(c * ra, 16), ra), :] = summed(0)
                    return

                def per_slot(i):
                    h, jj = 1 - i // (n // 2), i % (n // 2)
                    j = slot_at(c, s, h, jj)
                    ag[c, off[s - 1] + j] = summed(j).astype(BF16)

                    @pl.when(i < n // 2)
                    def _():
                        remote(ag.at[c, off[s - 1] + j], ag.at[c, off[s] + jj], send.at[3],
                               ag_r.at[c, s], across(c, s)).start()
                loop(n, per_slot)
            return body

        def b_first(c, t, slot):
            o = c % 2

            def per_slot(j):
                acc = product(slot, rb, group_at(o, 0, 1, j))
                bsend[c, t, j] = acc.astype(BF16)
                remote(bsend.at[c, t, j], bg.at[c, t, j], send.at[4], bg_r.at[c, t, 0], across(o, 0)).start()
            loop(half, per_slot)

        def b_merge(c, t, s, add):
            o = c % 2
            n = half >> (s - 1)
            arrived(bg.at[c, t, pl.ds(off[s - 1], n)], bg_r.at[c, t, s - 1])

            def per_slot(i):
                h, jj = 1 - i // (n // 2), i % (n // 2)
                j = slot_at(o, s, h, jj)
                bg[c, t, off[s - 1] + j] = (add(j) + bg[c, t, off[s - 1] + j].astype(F32)).astype(BF16)

                @pl.when(i < n // 2)
                def _():
                    remote(bg.at[c, t, off[s - 1] + j], bg.at[c, t, off[s] + jj], send.at[5],
                           bg_r.at[c, t, s], across(o, s)).start()
            loop(n, per_slot)

        def b_second(c, t, slot):
            b_merge(c, t, 1, lambda j: product(slot, rb, group_at(c % 2, 0, 0, j)))

        def b_middle(p, s):
            def body(i):
                c, t = 2 * p + i % 2, i // 2
                b_merge(c, t, s, lambda j: bg[c, t, off[s - 2] + slot_at(c % 2, s - 1, 0, j)].astype(F32))
            loop(2 * ring, body)

        def b_ring(p, t):
            def body(i):
                c = 2 * p + i
                last = off[bits - 1]
                arrived(bg.at[c, t, pl.ds(last, 1)], bg_r.at[c, t, bits - 1])
                kept = off[bits - 2] + slot_at(c % 2, bits - 1, 0, 0)
                val = bg[c, t, last].astype(F32) + bg[c, t, kept].astype(F32)
                if t > 0:
                    arrived(bz.at[c, t - 1], bz_r.at[c, t - 1])
                    val = val + bz[c, t - 1].astype(F32)
                if t == ring - 1:
                    out[0, pl.ds(pl.multiple_of(2 * ra + c * rb, 16), rb), :] = val
                    return
                if t == 0:
                    src = bg.at[c, t, last]
                    bg[c, t, last] = val.astype(BF16)
                else:
                    src = bz.at[c, t - 1]
                    bz[c, t - 1] = val.astype(BF16)
                remote(src, bz.at[c, t], send.at[6], bz_r.at[c, t], along(b_sign(c))).start()
            loop(2, body)

        def a_site(t, body):
            return ("tiles", True, True, 2, lambda i: (i, t), lambda c, t_, slot: body(c, slot))

        def b_site(p, first, body):
            return ("tiles", False, first, 2 * ring, lambda i: (2 * p + i % 2, i // 2), body)

        def plain(fn):
            return ("plain", fn)

        def b_tail(p):
            middle = [plain(lambda s=s: b_middle(p, s)) for s in range(2, bits)]
            return middle + [plain(lambda t=t: b_ring(p, t)) for t in range(ring)]

        a_queue = [a_site(t, a_hop(t)) for t in range(1, ring - 1)] + [a_site(ring - 1, a_turn)]
        a_queue += [plain(lambda s=s: loop(2, a_stage(s))) for s in range(1, bits + 1)]
        queues, order = [], [b_site(0, True, b_first), a_site(0, a_hop(0))]

        def drain():
            for q in queues:
                if q:
                    order.append(q.pop(0))

        for p in range(PAIRS):
            order.append(b_site(p, False, b_second))
            if p + 1 == PAIRS:
                break
            order.append(b_site(p + 1, True, b_first))
            queues.append(b_tail(p))
            drain()
            if len(a_queue) > bits + 1:
                order.append(a_queue.pop(0))
            drain()
        queues.append(b_tail(PAIRS - 1))
        while a_queue or any(queues):
            if a_queue:
                order.append(a_queue.pop(0))
            drain()

        def begin(site, i, slot):
            _, is_a, first, _, index, _ = site
            c, t = index(i)
            sgn = a_sign(c) if is_a else b_sign(c)
            own, other = tile_copies(is_a, c, t, sgn, slot)
            own.start()
            if is_a:
                arrived(wxa.at[c, t], wa_r.at[c, t])
            elif first:
                @pl.when(t == 0)
                def _():
                    arrived(wxb.at[c], wb_r.at[c])
            other.start()

        tiles = [s for s in order if s[0] == "tiles"]
        begin(tiles[0], 0, 0)
        at = 0
        for site in order:
            if site[0] == "plain":
                site[1]()
                continue
            at += 1
            follow = tiles[at] if at < len(tiles) else None
            _, is_a, first, count, index, body = site

            def run(i, site=site, follow=follow, is_a=is_a, count=count, index=index, body=body):
                slot = i % 2

                @pl.when(i + 1 < count)
                def _():
                    begin(site, i + 1, 1 - slot)

                if follow is not None:
                    @pl.when(i + 1 == count)
                    def _():
                        begin(follow, 0, 1 - slot)
                c, t = index(i)
                for cp in tile_copies(is_a, c, t, a_sign(c) if is_a else b_sign(c), slot):
                    cp.wait()
                body(c, t, slot)
            loop(count, run)

        x_copy.wait_send()
        arrived(wxa, w_s.at[0])
        arrived(wxb, w_s.at[1])
        arrived(asend, send.at[0])
        arrived(az.at[:, pl.ds(0, ring - 2)], send.at[1])
        arrived(ag.at[:, pl.ds(0, half)], send.at[2])
        arrived(ag.at[:, pl.ds(0, half - 1)], send.at[3])
        arrived(bsend, send.at[4])
        arrived(bg.at[:, :, pl.ds(0, half - 1)], send.at[5])
        arrived(bz, send.at[6])

    dma = pltpu.SemaphoreType.DMA
    nb = 2 * PAIRS
    shapes = [
        pltpu.VMEM((splits, depth, cols), BF16),
        pltpu.VMEM((groups, 2 * depth, cols), BF16),
        pltpu.VMEM((2, 2, blocks, max(ra, rb), depth), BF16),
        pltpu.VMEM((max(ra, rb), 2 * depth), BF16),
        pltpu.VMEM((2, groups, ra, cols), BF16),
        pltpu.VMEM((2, ring - 1, groups, ra, cols), BF16),
        pltpu.VMEM((2, groups - 1, ra, cols), BF16),
        pltpu.VMEM((nb, ring, half, rb, cols), BF16),
        pltpu.VMEM((nb, ring, groups - 1, rb, cols), BF16),
        pltpu.VMEM((nb, ring - 1, rb, cols), BF16),
        dma, dma, dma((2,)), dma((2, ring)), dma((nb,)), dma((2, 2)), dma((7,)),
        dma((2, ring - 1, groups)), dma((2, bits)), dma((nb, ring, bits)), dma((nb, ring - 1)),
    ]
    spaces = (pltpu.VMEM, pl.ANY, pl.ANY)
    return pl.pallas_call(
        kernel,
        name="coded_share",
        out_shape=(
            jax.ShapeDtypeStruct((1, rows, cols), F32),
            jax.ShapeDtypeStruct((2, ring, blocks, ra, depth), BF16),
            jax.ShapeDtypeStruct((nb, ring, blocks, rb, depth), BF16),
        ),
        in_specs=[
            pl.BlockSpec(memory_space=pltpu.SMEM),
            pl.BlockSpec(memory_space=pl.ANY),
            pl.BlockSpec(memory_space=pltpu.VMEM),
        ],
        out_specs=tuple(pl.BlockSpec(memory_space=m) for m in spaces),
        scratch_shapes=shapes,
        compiler_params=pltpu.CompilerParams(
            collective_id=0, has_side_effects=True, vmem_limit_bytes=67043328),
    )


def solution(mesh):
    groups, members = mesh.shape["grp"], mesh.shape["mem"]

    def per_device(weight, activation, points):
        blocks, height, depth = weight.shape
        splits, _, cols = activation.shape
        rows = height // members
        rb = (rows * 13 // 16) // (2 * PAIRS) // 16 * 16
        ra = (rows - 2 * PAIRS * rb) // 2
        call = make_kernel(groups, members, blocks, splits, rows, depth, cols, ra, rb)
        return call(points, weight, activation)[0]

    placed = (P(None, None, ("grp", "mem")), P(None, ("grp", "mem"), None), P())
    return jax.shard_map(
        per_device, mesh=mesh, in_specs=placed, out_specs=P("grp", "mem", None), check_vma=False)
```

profile of v0, /device:TPU:0, one launch (start us, length us, event | category | flops | bytes accessed | tf_op | source)
XLA Modules:
  0.0 273.9 jit_solution(4846884492180904871)
XLA Ops:
  0.0 269.3 %coded_share.1 = (f32[1,2048,512]{2,1,0:T(8,128)}, bf16[2,4,2,192,512]{4,3,2,1,0:T(8,128)(2,1)}, bf16[8,4,2,208,512]{4,3,2,1,0:T(8,128)(2,1)}) custom-call(s32[4]{0:T(128)} %points.1, bf16[2,16384,512]{2,1,0:T(8,128)(2,1)} %weight.1, bf16[2,512,512]{2,1,0:T(8,128)(2,1)} %act.1), custom_call_target="tpu_custom_call" | custom-call | tf_op jit(solution)/shard_map/coded_share/pallas_call | solution.py:419
  269.3 4.6 %copy.5 = f32[1,2048,512]{2,1,0:T(8,128)} copy(f32[1,2048,512]{2,1,0:T(8,128)} %get-tuple-element.6) | data formatting | bytes 8388608
where the time goes:
time: 275 us; the launch traced here: 274 us
  Pallas kernels  269 us (98%)
  local copies, waits for them, and re-layouts  4.64 us (2%)
    pallas_call x1, Pallas kernels, per_device(): return call(points, weight, activation)[0]  269 us

commit v1 on v0

v1 whole, which is shorter than its diff:
```python
import jax
import jax.numpy as jnp
from jax import lax
from jax.experimental import pallas as pl
from jax.experimental.pallas import tpu as pltpu
from jax.sharding import PartitionSpec as P

SHARE_A = 14
SHARES_B = (15, 15, 13, 7)
LIMIT = 58 * 1024 * 1024
UNITS_A = ((4, 2), (3, 2), (3, 3), (0, 0))
F32, BF16 = jnp.float32, jnp.bfloat16
MESH = pl.DeviceIdType.MESH


def loop(n, body):
    def step(i, carry):
        body(i)
        return carry

    lax.fori_loop(0, n, step, 0)


def blend(o, v0, v1):
    return v0 + o * (v1 - v0)


def choose(values, index):
    width = len(values)
    while width > 1:
        bit = index % 2
        values = [blend(bit, values[2 * i], values[2 * i + 1]) for i in range(width // 2)]
        index, width = index // 2, width // 2
    return values[0]


def line_order(n):
    table = []
    for z in range(n):
        def key(d):
            up = d > z
            slot = (n - 1 - d) + z if up else d + (n - 1 - z)
            return slot, up == (z < n // 2)
        table.append(sorted([d for d in range(n) if d != z], key=key) + [z])
    return table


def make_kernel(groups, members, blocks, splits, rows, depth, cols, ra, rbs):
    bits = groups.bit_length() - 1
    ring = members // 2
    half = groups // 2
    pairs = len(rbs)
    top = max([ra] + rbs)
    leads = [2 * ra + 2 * sum(rbs[:p]) for p in range(pairs)]
    off = [groups - (groups >> s) for s in range(bits + 1)]
    order_of = line_order(ring)
    n_units = 4 * ring

    def kernel(*refs):
        points, weight, act, out, wxa = refs[:5]
        wxb = refs[5:5 + pairs]
        refs = refs[5 + pairs:]
        (xo, xp, xs, wt, cw, accs, az, ag, bsend, x_s, x_r, x_o, w_s, wa_r, ld, send, b_s, az_r, ag_s, ag_r) = refs[:20]
        refs = refs[20:]
        bg, bz = refs[:pairs], refs[pairs:2 * pairs]
        wb_r, bg_r, bz_r = (refs[(2 + k) * pairs:(3 + k) * pairs] for k in range(3))

        me_g = lax.axis_index("grp")
        me_m = lax.axis_index("mem")
        z, core = me_m // 2, me_m % 2
        twin = (me_g, z * 2 + 1 - core)

        def bit_of(w):
            return (me_g // w) % 2

        def across(o, s):
            w0, w1 = 1 << (bits - 1 - s), 1 << s
            p0 = me_g + w0 - 2 * w0 * bit_of(w0)
            p1 = me_g + w1 - 2 * w1 * bit_of(w1)
            return (blend(o, p0, p1), me_m)

        def group_at(o, s, h, j):
            w0, w1 = 1 << (bits - 1 - s), 1 << s
            b0, b1 = bit_of(w0), bit_of(w1)
            b0, b1 = b0 + h - 2 * b0 * h, b1 + h - 2 * b1 * h
            g0 = (me_g // (2 * w0)) * (2 * w0) + b0 * w0 + j
            g1 = me_g % w1 + b1 * w1 + j * (2 * w1)
            return blend(o, g0, g1)

        def slot_at(o, s, h, j):
            w0, w1 = 1 << (bits - 1 - s), 1 << s
            b0, b1 = bit_of(w0), bit_of(w1)
            b0, b1 = b0 + h - 2 * b0 * h, b1 + h - 2 * b1 * h
            return blend(o, b0 * w0 + j, b1 + 2 * j)

        def remote(src, dst, ssem, rsem, dev):
            return pltpu.make_async_remote_copy(
                src_ref=src, dst_ref=dst, send_sem=ssem, recv_sem=rsem, device_id=dev, device_id_type=MESH)

        def arrived(ref, sem):
            pltpu.make_async_copy(ref, ref, sem).wait()

        def anchor(g):
            return (points[g] + 1).astype(F32) / groups

        def power(a, n):
            r = a
            for _ in range(n - 1):
                r = r * a
            return r

        def per_place(fn):
            return [choose([fn(q, order_of[q][t]) for q in range(ring)], z) for t in range(ring)]

        def landing(q, d):
            if d == q:
                return d
            return ring if d == q - 1 else d

        dests = per_place(lambda q, d: d)
        signs = per_place(lambda q, d: 1 if d > q else -1)
        feeds = per_place(lambda q, d: int(d != q and 0 <= q - (1 if d > q else -1) < ring))
        lands = per_place(landing)
        left, right = z > 0, z < ring - 1
        ends = choose([int(q in (0, ring - 1)) for q in range(ring)], z)

        def dest(t):
            return dests[t] if isinstance(t, int) else choose(dests, t)

        def toward(t):
            return (me_g, (z + choose(signs, t)) * 2 + core)

        barrier = pltpu.get_barrier_semaphore()
        peers = [twin] + [across(0, s) for s in range(bits)]
        for dev in peers:
            pl.semaphore_signal(barrier, inc=1, device_id=dev, device_id_type=MESH)
        for there, sgn in ((left, -1), (right, 1)):
            @pl.when(there)
            def _(sgn=sgn):
                pl.semaphore_signal(barrier, inc=1, device_id=(me_g, (z + sgn) * 2 + core), device_id_type=MESH)

        def meet():
            beside = choose([int(q > 0) + int(q < ring - 1) for q in range(ring)], z)
            pl.semaphore_wait(barrier, len(peers) + beside)

        x_own = pltpu.make_async_copy(act, xo, x_o)
        x_own.start()

        def base(lead, d, core_):
            return pl.multiple_of((d * 2 + core_) * rows + lead, 16)

        x_copy = remote(act, xp, x_s, x_r, twin)

        def push_a(c, t):
            remote(weight.at[:, pl.ds(base(c * ra, dest(t), 1 - core), ra), :], wxa.at[c, t],
                   w_s.at[pairs], wa_r.at[c, t], twin).start()

        def push_b(p, c, t):
            rb = rbs[p]
            remote(weight.at[:, pl.ds(base(leads[p] + c * rb, dest(t), 1 - core), rb), :], wxb[p].at[c, t],
                   w_s.at[p], wb_r[p].at[c, t], twin).start()

        def push_both(p):
            def body(i):
                push_b(p, i % 2, i // 2)
            loop(2 * ring, body)

        def push_first(t):
            push_a(0, t)
            push_b(0, 0, t)
            push_b(0, 1, t)

        step = min(16, depth)
        lifts = [power(anchor(g), blocks) for g in range(groups)]

        def code_input(h, src):
            def body(r):
                at = pl.ds(pl.multiple_of(r * step, step), step)
                to = pl.ds(pl.multiple_of(h * depth + r * step, step), step)
                parts = [src[k, at, :].astype(F32) for k in range(splits)]
                for g in range(groups):
                    total = parts[0]
                    for k in range(1, splits):
                        total = total + power(lifts[g], k) * parts[k]
                    xs[g, to, :] = total.astype(BF16)
            loop(depth // step, body)

        meet()
        x_copy.start()
        loop(ring, push_first)
        x_own.wait()
        code_input(0, xo)

        def tile_copies(lead, d, n, there, slot):
            own = pltpu.make_async_copy(
                weight.at[:, pl.ds(base(lead, d, core), n), :], wt.at[slot, 0, :, pl.ds(0, n), :], ld.at[slot, 0])
            other = pltpu.make_async_copy(there, wt.at[slot, 1, :, pl.ds(0, n), :], ld.at[slot, 1])
            return own, other

        def product(slot, n, g):
            a = anchor(g)
            factors = [power(a, j) for j in range(1, blocks)]

            def body(r):
                at = pl.ds(r * 16, 16)
                for h in range(2):
                    total = wt[slot, h, 0, at, :].astype(F32)
                    for j in range(1, blocks):
                        total = total + factors[j - 1] * wt[slot, h, j, at, :].astype(F32)
                    cw[at, h * depth:(h + 1) * depth] = total.astype(BF16)
            for r in range(n // 16):
                body(r)
            return jnp.dot(cw[0:n, :], xs[g], preferred_element_type=F32)

        def a_unit(u):
            return u // (2 * ring), (u // 2) % ring, u % 2

        def a_body(u, slot):
            c, t, hh = a_unit(u)
            d, feed = dest(t), choose(feeds, t)
            last = t == ring - 1

            def per_group(j):
                g = group_at(c, 0, 1 - hh, j)
                accs[0:ra, :] = product(slot, ra, g)

                def take(there, at):
                    @pl.when(there)
                    def _():
                        arrived(az.at[c, at, g], az_r.at[c, at, g])
                        accs[0:ra, :] = accs[0:ra, :] + az[c, at, g].astype(F32)

                take(jnp.logical_or(feed == 1, jnp.logical_and(last, left)), d)
                take(jnp.logical_and(last, right), ring)
                az[c, d, g] = accs[0:ra, :].astype(BF16)

                @pl.when(t < ring - 1)
                def _():
                    land = choose(lands, t)
                    remote(az.at[c, d, g], az.at[c, land, g], send.at[0], az_r.at[c, land, g], toward(t)).start()
            loop(half, per_group)

        def a_spread(c):
            n = half // 2

            def per_slot(i):
                j = slot_at(c, 1, 1 - i // n, i % n)
                g = group_at(c, 0, 1, j)
                remote(az.at[c, z, g], ag.at[c, j], send.at[1], ag_s.at[c, j], across(c, 0)).start()
            loop(half, per_slot)

        def a_held(s, c, j):
            if s == 1:
                return az[c, z, group_at(c, 0, 0, j)]
            return ag[c, off[s - 2] + slot_at(c, s - 1, 0, j)]

        def a_sum(s, c, j):
            return ag[c, off[s - 1] + j].astype(F32) + a_held(s, c, j).astype(F32)

        def a_part(s, c, h):
            n = half >> s

            def per_slot(jj):
                j = slot_at(c, s, h, jj)
                if s == 1:
                    arrived(ag.at[c, j], ag_s.at[c, j])
                ag[c, off[s - 1] + j] = a_sum(s, c, j).astype(BF16)
                if h == 1:
                    remote(ag.at[c, off[s - 1] + j], ag.at[c, off[s] + jj], send.at[2],
                           ag_r.at[c, s], across(c, s)).start()
            loop(n, per_slot)

        def a_send(s, c):
            if s > 1:
                arrived(ag.at[c, pl.ds(off[s - 1], half >> (s - 1))], ag_r.at[c, s - 1])
            a_part(s, c, 1)

        def a_keep(s, c):
            a_part(s, c, 0)

        def a_close(c):
            arrived(ag.at[c, pl.ds(off[bits - 1], 1)], ag_r.at[c, bits - 1])
            out[0, pl.ds(pl.multiple_of(c * ra, 16), ra), :] = a_sum(bits, c, 0)

        def b_first(p, c, t, slot):
            rb, q = rbs[p], p % 2

            def per_slot(j):
                acc = product(slot, rb, group_at(c, 0, 1, j))
                src = bsend.at[q, c, t, j, pl.ds(0, rb), :]
                src[...] = acc.astype(BF16)
                remote(src, bg[p].at[c, t, j], b_s.at[q], bg_r[p].at[c, t, 0], across(c, 0)).start()
            loop(half, per_slot)

        def b_sent(p):
            q = p % 2
            arrived(bsend.at[q, :, :, :, pl.ds(0, rbs[p]), :], b_s.at[q])

        def b_merge(p, c, t, s, add):
            n = half >> (s - 1)
            arrived(bg[p].at[c, t, pl.ds(off[s - 1], n)], bg_r[p].at[c, t, s - 1])

            def per_slot(i):
                h, jj = 1 - i // (n // 2), i % (n // 2)
                j = slot_at(c, s, h, jj)
                bg[p][c, t, off[s - 1] + j] = (add(j) + bg[p][c, t, off[s - 1] + j].astype(F32)).astype(BF16)

                @pl.when(i < n // 2)
                def _():
                    remote(bg[p].at[c, t, off[s - 1] + j], bg[p].at[c, t, off[s] + jj], send.at[3],
                           bg_r[p].at[c, t, s], across(c, s)).start()
            loop(n, per_slot)

        def b_second(p, c, t, slot):
            b_merge(p, c, t, 1, lambda j: product(slot, rbs[p], group_at(c, 0, 0, j)))

        def b_middle(p, t):
            for s in range(2, bits):
                loop(2, lambda c: b_merge(
                    p, c, t, s, lambda j: bg[p][c, t, off[s - 2] + slot_at(c, s - 1, 0, j)].astype(F32)))

        def b_line(p, t):
            rb = rbs[p]
            d = dest(t)

            def body(c):
                tail = off[bits - 1]
                arrived(bg[p].at[c, t, pl.ds(tail, 1)], bg_r[p].at[c, t, bits - 1])
                kept = off[bits - 2] + slot_at(c, bits - 1, 0, 0)

                def val():
                    return bg[p][c, t, tail].astype(F32) + bg[p][c, t, kept].astype(F32)

                feed = choose(feeds, t)
                mid = t < ring - 1

                @pl.when(jnp.logical_and(mid, feed == 0))
                def _():
                    bz[p][c, d] = val().astype(BF16)

                @pl.when(jnp.logical_and(mid, feed == 1))
                def _():
                    arrived(bz[p].at[c, d], bz_r[p].at[c, d])
                    bz[p][c, d] = (val() + bz[p][c, d].astype(F32)).astype(BF16)

                @pl.when(mid)
                def _():
                    land = choose(lands, t)
                    remote(bz[p].at[c, d], bz[p].at[c, land], send.at[4], bz_r[p].at[c, land], toward(t)).start()

                @pl.when(t == ring - 1)
                def _():
                    at = pl.ds(pl.multiple_of(leads[p] + c * rb, 16), rb)
                    out[0, at, :] = val()
                    for there, slot in ((left, z), (right, ring)):
                        @pl.when(there)
                        def _():
                            arrived(bz[p].at[c, slot], bz_r[p].at[c, slot])
                            out[0, at, :] = out[0, at, :] + bz[p][c, slot].astype(F32)
            loop(2, body)

        class Tiles:
            def __init__(self, count, spot, body, first=None, valid=None):
                self.count, self.spot, self.body, self.first = count, spot, body, first
                self.valid = valid or (lambda i: None)

            def guard(self, i, fn):
                ok = self.valid(i)
                if ok is None:
                    fn()
                else:
                    pl.when(ok)(fn)

            def begin(self, i, j, slot):
                def go():
                    own, other = tile_copies(*self.spot(i, j), slot)
                    own.start()
                    if self.first is not None:
                        self.first(i, j)
                    other.start()
                self.guard(i, go)

            def run(self, i, j, slot):
                def go():
                    for cp in tile_copies(*self.spot(i, j), slot):
                        cp.wait()
                    self.body(i, j, slot)
                self.guard(i, go)

        def b_tiles(p, first):
            rb = rbs[p]

            def spot(i, j):
                return leads[p] + j * rb, dest(i), rb, wxb[p].at[j, i]

            def await_rows(i, j):
                arrived(wxb[p].at[j, i], wb_r[p].at[j, i])

            fn = b_first if first else b_second
            return Tiles(2, spot, lambda i, j, slot: fn(p, j, i, slot), await_rows if first else None)

        def a_tiles(k0, amount, count):
            def unit(i):
                return k0 + (i * amount) // count - 1 + 2 * ends

            def spot(i, j):
                c, t, _ = a_unit(unit(i))
                return c * ra, dest(t), ra, wxa.at[c, t]

            def await_rows(i, j):
                c, t, hh = a_unit(unit(i))

                @pl.when(hh == 0)
                def _():
                    arrived(wxa.at[c, t], wa_r.at[c, t])

            def valid(i):
                u = unit(i)
                ok = jnp.logical_and(u >= 0, u < n_units)
                return jnp.logical_and(ok, ((i + 1) * amount) // count > (i * amount) // count)

            return Tiles(1, spot, lambda i, j, slot: a_body(unit(i), slot), await_rows, valid)

        def z_step(p, t):
            b_middle(p, t)
            b_line(p, t)

        early = a_tiles(-1, 1, 1)
        early.begin(0, 0, 0)
        b_tiles(0, True).begin(0, 0, 1)
        x_copy.wait_recv()
        code_input(1, xp)
        early.run(0, 0, 0)
        push_both(1)
        loop(ring, lambda t: push_a(1, t))
        for p in range(2, pairs):
            push_both(p)

        sites = []
        k0 = 0
        for p in range(pairs):
            final = p == pairs - 1
            for first in (True, False):
                amount = UNITS_A[p][0 if first else 1] * ring // 4
                parts = [b_tiles(p, first)]
                if amount:
                    parts.append(a_tiles(k0, amount, ring))
                    k0 += amount
                post = None
                if first and p >= 2:
                    sites.append(lambda p=p: b_sent(p - 2))
                if not first and p >= 1:
                    def post(i, p=p, final=final):
                        t = blend(ends, i - 1, i + 1)
                        ok = jnp.logical_and(t >= 0, t < ring - 1)

                        @pl.when(jnp.logical_and(ok, ends == 0) if final else ok)
                        def _():
                            z_step(p - 1, t)
                sites.append((ring, parts, post))
                if first and p >= 2:
                    sites.append(lambda p=p: z_step(p - 2, ring - 1))
                if first and p >= 1:
                    def lead_on(p=p, final=final):
                        @pl.when(ends == 1)
                        def _():
                            loop(ring - 1 if final else 1, lambda t: z_step(p - 1, t))
                    sites.append(lead_on)

        def tail():
            last = pairs - 1
            a_spread(0)
            a_spread(1)
            loop(ring - 2, lambda t: z_step(last, t))
            for c in range(2):
                a_send(1, c)
            z_step(last, ring - 2)
            for c in range(2):
                a_keep(1, c)
            z_step(last - 1, ring - 1)
            for s in range(2, bits):
                for c in range(2):
                    a_send(s, c)
                    a_keep(s, c)
            z_step(last, ring - 1)
            for c in range(2):
                a_close(c)

        sites.append(tail)

        tiled = [site for site in sites if isinstance(site, tuple)]
        seen, parity = 0, 1
        for site in sites:
            if not isinstance(site, tuple):
                site()
                continue
            seen += 1
            follow = tiled[seen][1][0] if seen < len(tiled) else None
            count, parts, post = site
            per = sum(part.count for part in parts)

            def run(i, count=count, parts=parts, post=post, per=per, follow=follow, parity=parity):
                lead = 0
                for q, part in enumerate(parts):
                    def visit(j, q=q, part=part, lead=lead):
                        slot = (parity + i * per + lead + j) % 2

                        @pl.when(j + 1 < part.count)
                        def _():
                            part.begin(i, j + 1, 1 - slot)

                        @pl.when(j + 1 == part.count)
                        def _():
                            if q + 1 < len(parts):
                                parts[q + 1].begin(i, 0, 1 - slot)
                                return

                            @pl.when(i + 1 < count)
                            def _():
                                parts[0].begin(i + 1, 0, 1 - slot)
                            if follow is not None:
                                @pl.when(i + 1 == count)
                                def _():
                                    follow.begin(0, 0, 1 - slot)
                        part.run(i, j, slot)
                    loop(part.count, visit)
                    lead += part.count
                if post is not None:
                    post(i)
            loop(count, run)
            parity = (parity + count * per) % 2

        x_copy.wait_send()
        for p in range(pairs):
            arrived(wxb[p], w_s.at[p])
        arrived(wxa, w_s.at[pairs])
        arrived(az.at[:, pl.ds(0, ring - 1)], send.at[0])
        arrived(ag.at[:, pl.ds(0, half)], send.at[1])
        arrived(ag.at[:, pl.ds(0, half - 1)], send.at[2])
        for p in range(max(0, pairs - 2), pairs):
            b_sent(p)
        for p in range(pairs):
            arrived(bg[p].at[:, :, pl.ds(0, half - 1)], send.at[3])
            arrived(bz[p].at[:, pl.ds(0, ring - 1)], send.at[4])

    dma = pltpu.SemaphoreType.DMA
    shapes = [
        pltpu.VMEM((splits, depth, cols), BF16),
        pltpu.VMEM((splits, depth, cols), BF16),
        pltpu.VMEM((groups, 2 * depth, cols), BF16),
        pltpu.VMEM((2, 2, blocks, top, depth), BF16),
        pltpu.VMEM((top, 2 * depth), BF16),
        pltpu.VMEM((top, cols), F32),
        pltpu.VMEM((2, ring + 1, groups, ra, cols), BF16),
        pltpu.VMEM((2, groups - 1, ra, cols), BF16),
        pltpu.VMEM((2, 2, ring, half, max(rbs), cols), BF16),
        dma, dma, dma, dma((pairs + 1,)), dma((2, ring)), dma((2, 2)), dma((5,)), dma((2,)),
        dma((2, ring + 1, groups)), dma((2, half)), dma((2, bits)),
    ]
    shapes += [pltpu.VMEM((2, ring, groups - 1, rb, cols), BF16) for rb in rbs]
    shapes += [pltpu.VMEM((2, ring + 1, rb, cols), BF16) for rb in rbs]
    shapes += [dma((2, ring)) for _ in rbs]
    shapes += [dma((2, ring, bits)) for _ in rbs]
    shapes += [dma((2, ring + 1)) for _ in rbs]
    held = [jax.ShapeDtypeStruct((2, ring, blocks, ra, depth), BF16)]
    held += [jax.ShapeDtypeStruct((2, ring, blocks, rb, depth), BF16) for rb in rbs]
    return pl.pallas_call(
        kernel,
        name="coded_share",
        out_shape=(pltpu.VMEM((1, rows, cols), F32), *held),
        in_specs=[
            pl.BlockSpec(memory_space=pltpu.SMEM),
            pl.BlockSpec(memory_space=pl.ANY),
            pl.BlockSpec(memory_space=pl.ANY),
        ],
        out_specs=tuple(pl.BlockSpec(memory_space=m) for m in [pltpu.VMEM] + [pl.ANY] * len(held)),
        scratch_shapes=shapes,
        compiler_params=pltpu.CompilerParams(
            collective_id=0, has_side_effects=True, vmem_limit_bytes=LIMIT),
    )


def split_rows(rows):
    units = rows // 16
    ua = max(1, units * SHARE_A // 128)
    ub = (units - 2 * ua) // 2
    whole = sum(SHARES_B)
    cut = [max(1, ub * share // whole) for share in SHARES_B]
    for i in range(ub - sum(cut)):
        cut[i % len(cut)] += 1
    return 16 * ua, [16 * n for n in cut]


def solution(mesh):
    groups, members = mesh.shape["grp"], mesh.shape["mem"]

    def per_device(weight, activation, points):
        blocks, height, depth = weight.shape
        splits, _, cols = activation.shape
        rows = height // members
        ra, rbs = split_rows(rows)
        call = make_kernel(groups, members, blocks, splits, rows, depth, cols, ra, rbs)
        return call(points, weight, activation)[0]

    placed = (P(None, None, ("grp", "mem")), P(None, ("grp", "mem"), None), P())
    return jax.shard_map(
        per_device, mesh=mesh, in_specs=placed, out_specs=P("grp", "mem", None), check_vma=False)
```

time: 275 us -> 245 us (0.89)
  Pallas kernels: 269 us -> 241 us
    pallas_call x1, Pallas kernels: 269 us -> 241 us  [per_device(): return call(points, weight, activation)[0]]
where the time goes in v1:
time: 245 us; the launch traced here: 243 us
  Pallas kernels  241 us (98%)
    pallas_call x1, Pallas kernels, per_device(): return call(points, weight, activation)[0]  241 us

profile of v1, /device:TPU:0, one launch (start us, length us, event | category | flops | bytes accessed | tf_op | source)
XLA Modules:
  0.0 243.4 jit_solution(16337444879583401257)
XLA Ops:
  0.0 241.4 %coded_share.1 = (f32[1,2048,512]{2,1,0:T(8,128)S(1)}, bf16[2,4,2,224,512]{4,3,2,1,0:T(8,128)(2,1)}, bf16[2,4,2,240,512]{4,3,2,1,0:T(8,128)(2,1)}, bf16[2,4,2,24...) custom-call(s32[4]{0:T(128)} %refs_0_.1, ...), custom_call_target="tpu_custom_call" | custom-call | tf_op jit(solution)/shard_map/coded_share/pallas_call | solution.py:603
  241.4 2.0 copy.5

commit v2 on v1

--- a/solution.py
+++ b/solution.py
@@ -8,7 +8,7 @@
 SHARE_A = 14
 SHARES_B = (15, 15, 13, 7)
 LIMIT = 58 * 1024 * 1024
-UNITS_A = ((4, 2), (3, 2), (3, 3), (0, 0))
+UNITS_A = ((4, 3), (3, 2), (3, 3), (0, 0))
 F32, BF16 = jnp.float32, jnp.bfloat16
 MESH = pl.DeviceIdType.MESH
 
@@ -60,8 +60,8 @@
         points, weight, act, out, wxa = refs[:5]
         wxb = refs[5:5 + pairs]
         refs = refs[5 + pairs:]
-        (xo, xp, xs, wt, cw, accs, az, ag, bsend, x_s, x_r, x_o, w_s, wa_r, ld, send, b_s, az_r, ag_s, ag_r) = refs[:20]
-        refs = refs[20:]
+        (xo, xp, stage, xs, wt, cw, accs, az, ag, bsend, x_s, x_r, x_o, st_l, st_s, st_r, w_s, wa_r, ld, send, b_s, az_r, ag_s, ag_r) = refs[:24]
+        refs = refs[24:]
         bg, bz = refs[:pairs], refs[pairs:2 * pairs]
         wb_r, bg_r, bz_r = (refs[(2 + k) * pairs:(3 + k) * pairs] for k in range(3))
 
@@ -129,6 +129,29 @@
 
         def toward(t):
             return (me_g, (z + choose(signs, t)) * 2 + core)
+
+        def base(lead, d, core_):
+            return pl.multiple_of((d * 2 + core_) * rows + lead, 16)
+
+        def tile_own(lead, d, n, there, slot):
+            return pltpu.make_async_copy(
+                weight.at[:, pl.ds(base(lead, d, core), n), :], wt.at[slot, 0, :, pl.ds(0, n), :], ld.at[slot, 0])
+
+        def tile_other(lead, d, n, there, slot):
+            return pltpu.make_async_copy(there, wt.at[slot, 1, :, pl.ds(0, n), :], ld.at[slot, 1])
+
+        def stage_load(c):
+            rb = rbs[0]
+            return pltpu.make_async_copy(
+                weight.at[:, pl.ds(base(leads[0] + c * rb, dest(0), 1 - core), rb), :], stage.at[c], st_l.at[c])
+
+        def stage_give(c):
+            return remote(stage.at[c], wt.at[c, 1, :, pl.ds(0, rbs[0]), :], st_s.at[c], st_r.at[c], twin)
+
+        def begin_first():
+            for c in range(2):
+                stage_load(c).start()
+                tile_own(leads[0] + c * rbs[0], dest(0), rbs[0], None, c).start()
 
         barrier = pltpu.get_barrier_semaphore()
         peers = [twin] + [across(0, s) for s in range(bits)]
@@ -145,11 +168,9 @@
 
         x_own = pltpu.make_async_copy(act, xo, x_o)
         x_own.start()
-
-        def base(lead, d, core_):
-            return pl.multiple_of((d * 2 + core_) * rows + lead, 16)
-
-        x_copy = remote(act, xp, x_s, x_r, twin)
+        begin_first()
+
+        x_copy = remote(xo, xp, x_s, x_r, twin)
 
         def push_a(c, t):
             remote(weight.at[:, pl.ds(base(c * ra, dest(t), 1 - core), ra), :], wxa.at[c, t],
@@ -167,8 +188,8 @@
 
         def push_first(t):
             push_a(0, t)
-            push_b(0, 0, t)
-            push_b(0, 1, t)
+            push_b(0, 0, (t + 1) % ring)
+            push_b(0, 1, (t + 1) % ring)
 
         step = min(16, depth)
         lifts = [power(anchor(g), blocks) for g in range(groups)]
@@ -185,17 +206,15 @@
                     xs[g, to, :] = total.astype(BF16)
             loop(depth // step, body)
 
+        x_own.wait()
+        code_input(0, xo)
+        for c in range(2):
+            stage_load(c).wait()
         meet()
         x_copy.start()
+        for c in range(2):
+            stage_give(c).start()
         loop(ring, push_first)
-        x_own.wait()
-        code_input(0, xo)
-
-        def tile_copies(lead, d, n, there, slot):
-            own = pltpu.make_async_copy(
-                weight.at[:, pl.ds(base(lead, d, core), n), :], wt.at[slot, 0, :, pl.ds(0, n), :], ld.at[slot, 0])
-            other = pltpu.make_async_copy(there, wt.at[slot, 1, :, pl.ds(0, n), :], ld.at[slot, 1])
-            return own, other
 
         def product(slot, n, g):
             a = anchor(g)
@@ -282,15 +301,15 @@
             arrived(ag.at[c, pl.ds(off[bits - 1], 1)], ag_r.at[c, bits - 1])
             out[0, pl.ds(pl.multiple_of(c * ra, 16), ra), :] = a_sum(bits, c, 0)
 
+        def b_one(p, c, t, slot, j):
+            rb, q = rbs[p], p % 2
+            acc = product(slot, rb, group_at(c, 0, 1, j))
+            src = bsend.at[q, c, t, j, pl.ds(0, rb), :]
+            src[...] = acc.astype(BF16)
+            remote(src, bg[p].at[c, t, j], b_s.at[q], bg_r[p].at[c, t, 0], across(c, 0)).start()
+
         def b_first(p, c, t, slot):
-            rb, q = rbs[p], p % 2
-
-            def per_slot(j):
-                acc = product(slot, rb, group_at(c, 0, 1, j))
-                src = bsend.at[q, c, t, j, pl.ds(0, rb), :]
-                src[...] = acc.astype(BF16)
-                remote(src, bg[p].at[c, t, j], b_s.at[q], bg_r[p].at[c, t, 0], across(c, 0)).start()
-            loop(half, per_slot)
+            loop(half, lambda j: b_one(p, c, t, slot, j))
 
         def b_sent(p):
             q = p % 2
@@ -373,35 +392,38 @@
 
             def begin(self, i, j, slot):
                 def go():
-                    own, other = tile_copies(*self.spot(i, j), slot)
-                    own.start()
+                    tile_own(*self.spot(i, j), slot).start()
                     if self.first is not None:
                         self.first(i, j)
-                    other.start()
+                    tile_other(*self.spot(i, j), slot).start()
                 self.guard(i, go)
 
             def run(self, i, j, slot):
                 def go():
-                    for cp in tile_copies(*self.spot(i, j), slot):
-                        cp.wait()
+                    tile_own(*self.spot(i, j), slot).wait()
+                    tile_other(*self.spot(i, j), slot).wait()
                     self.body(i, j, slot)
                 self.guard(i, go)
 
-        def b_tiles(p, first):
+        def b_tiles(p, first, t0=0):
             rb = rbs[p]
+            fn = b_first if first else b_second
 
             def spot(i, j):
-                return leads[p] + j * rb, dest(i), rb, wxb[p].at[j, i]
+                return leads[p] + j * rb, dest(t0 + i), rb, wxb[p].at[j, t0 + i]
 
             def await_rows(i, j):
-                arrived(wxb[p].at[j, i], wb_r[p].at[j, i])
-
-            fn = b_first if first else b_second
-            return Tiles(2, spot, lambda i, j, slot: fn(p, j, i, slot), await_rows if first else None)
+                arrived(wxb[p].at[j, t0 + i], wb_r[p].at[j, t0 + i])
+
+            def await_laid(i, j):
+                pl.when(i == 0)(lambda: await_rows(i, j))
+
+            await_fn = await_rows if first else await_laid if p == 0 else None
+            return Tiles(2, spot, lambda i, j, slot: fn(p, j, t0 + i, slot), await_fn)
 
         def a_tiles(k0, amount, count):
             def unit(i):
-                return k0 + (i * amount) // count - 1 + 2 * ends
+                return k0 + (i * amount) // count - 2 + 2 * ends
 
             def spot(i, j):
                 c, t, _ = a_unit(unit(i))
@@ -425,56 +447,76 @@
             b_middle(p, t)
             b_line(p, t)
 
-        early = a_tiles(-1, 1, 1)
-        early.begin(0, 0, 0)
-        b_tiles(0, True).begin(0, 0, 1)
         x_copy.wait_recv()
         code_input(1, xp)
-        early.run(0, 0, 0)
-        push_both(1)
-        loop(ring, lambda t: push_a(1, t))
-        for p in range(2, pairs):
-            push_both(p)
-
-        sites = []
-        k0 = 0
+        def laid(c):
+            tile_own(leads[0] + c * rbs[0], dest(0), rbs[0], None, c).wait()
+            arrived(wt.at[c, 1, :, pl.ds(0, rbs[0]), :], st_r.at[c])
+
+        laid(0)
+        b_one(0, 0, 0, 0, 0)
+        laid(1)
+        b_one(0, 1, 0, 1, 0)
+        loop(half - 1, lambda j: b_one(0, 0, 0, 0, j + 1))
+        opening = a_tiles(0, 1, 1)
+        opening.begin(0, 0, 0)
+        loop(half - 1, lambda j: b_one(0, 1, 0, 1, j + 1))
+
+        def push_rest():
+            push_both(1)
+            loop(ring, lambda t: push_a(1, t))
+            for p in range(2, pairs):
+                push_both(p)
+
+        sites = [(1, [opening], None), push_rest]
+        k0 = 1
         for p in range(pairs):
             final = p == pairs - 1
             for first in (True, False):
                 amount = UNITS_A[p][0 if first else 1] * ring // 4
-                parts = [b_tiles(p, first)]
+                lead_in = int(p == 0 and first)
+                amount -= lead_in
+                count = ring - lead_in
+                parts = [b_tiles(p, first, lead_in)]
                 if amount:
-                    parts.append(a_tiles(k0, amount, ring))
+                    parts.append(a_tiles(k0, amount, count))
                     k0 += amount
                 post = None
                 if first and p >= 2:
                     sites.append(lambda p=p: b_sent(p - 2))
                 if not first and p >= 1:
                     def post(i, p=p, final=final):
-                        t = blend(ends, i - 1, i + 1)
+                        t = i if final else blend(ends, i - 1, i + 1)
                         ok = jnp.logical_and(t >= 0, t < ring - 1)
 
                         @pl.when(jnp.logical_and(ok, ends == 0) if final else ok)
                         def _():
                             z_step(p - 1, t)
-                sites.append((ring, parts, post))
-                if first and p >= 2:
-                    sites.append(lambda p=p: z_step(p - 2, ring - 1))
+                sites.append((count, parts, post))
                 if first and p >= 1:
                     def lead_on(p=p, final=final):
                         @pl.when(ends == 1)
                         def _():
                             loop(ring - 1 if final else 1, lambda t: z_step(p - 1, t))
                     sites.append(lead_on)
+                if first and p >= 2:
+                    sites.append(lambda p=p: z_step(p - 2, ring - 1))
 
         def tail():
             last = pairs - 1
             a_spread(0)
             a_spread(1)
-            loop(ring - 2, lambda t: z_step(last, t))
+            z_step(last, 0)
+
+            def pass_on(mine):
+                @pl.when(ends == mine)
+                def _():
+                    loop(ring - 2, lambda t: z_step(last, t + 1))
+
+            pass_on(1)
             for c in range(2):
                 a_send(1, c)
-            z_step(last, ring - 2)
+            pass_on(0)
             for c in range(2):
                 a_keep(1, c)
             z_step(last - 1, ring - 1)
@@ -489,7 +531,7 @@
         sites.append(tail)
 
         tiled = [site for site in sites if isinstance(site, tuple)]
-        seen, parity = 0, 1
+        seen, parity = 0, 0
         for site in sites:
             if not isinstance(site, tuple):
                 site()
@@ -534,6 +576,8 @@
         for p in range(pairs):
             arrived(wxb[p], w_s.at[p])
         arrived(wxa, w_s.at[pairs])
+        for c in range(2):
+            arrived(stage.at[c], st_s.at[c])
         arrived(az.at[:, pl.ds(0, ring - 1)], send.at[0])
         arrived(ag.at[:, pl.ds(0, half)], send.at[1])
         arrived(ag.at[:, pl.ds(0, half - 1)], send.at[2])
@@ -547,6 +591,7 @@
     shapes = [
         pltpu.VMEM((splits, depth, cols), BF16),
         pltpu.VMEM((splits, depth, cols), BF16),
+        pltpu.VMEM((2, blocks, rbs[0], depth), BF16),
         pltpu.VMEM((groups, 2 * depth, cols), BF16),
         pltpu.VMEM((2, 2, blocks, top, depth), BF16),
         pltpu.VMEM((top, 2 * depth), BF16),
@@ -554,7 +599,7 @@
         pltpu.VMEM((2, ring + 1, groups, ra, cols), BF16),
         pltpu.VMEM((2, groups - 1, ra, cols), BF16),
         pltpu.VMEM((2, 2, ring, half, max(rbs), cols), BF16),
-        dma, dma, dma, dma((pairs + 1,)), dma((2, ring)), dma((2, 2)), dma((5,)), dma((2,)),
+        dma, dma, dma, dma((2,)), dma((2,)), dma((2,)), dma((pairs + 1,)), dma((2, ring)), dma((2, 2)), dma((5,)), dma((2,)),
         dma((2, ring + 1, groups)), dma((2, half)), dma((2, bits)),
     ]
     shapes += [pltpu.VMEM((2, ring, groups - 1, rb, cols), BF16) for rb in rbs]

time: 245 us -> 242 us (0.988)
    pallas_call x1, Pallas kernels: 241 us -> 239 us  [per_device(): return call(points, weight, activation)[0]]
where the time goes in v2:
time: 242 us; the launch traced here: 241 us
  Pallas kernels  239 us (99%)
    pallas_call x1, Pallas kernels, per_device(): return call(points, weight, activation)[0]  239 us

profile of v2, /device:TPU:0, one launch (start us, length us, event | category | flops | bytes accessed | tf_op | source)
XLA Modules:
  0.0 240.7 jit_solution(12760436688246001424)
XLA Ops:
  0.0 238.7 %coded_share.1 = (f32[1,2048,512]{2,1,0:T(8,128)S(1)}, bf16[2,4,2,224,512]{4,3,2,1,0:T(8,128)(2,1)}, bf16[2,4,2,240,512]{4,3,2,1,0:T(8,128)(2,1)}, bf16[2,4,2,24...) custom-call(s32[4]{0:T(128)} %refs_0_.1, ...), custom_call_target="tpu_custom_call" | custom-call | tf_op jit(solution)/shard_map/coded_share/pallas_call | solution.py:648
  238.7 2.0 copy.5
